TPU v7x, 32 devices: a whole 2x2x4 slice. The times are simulated.
32 devices in a mesh: seq: 8 (over y, x, core), tp: 4 (over z).
Axes of the slice: x: 2, y: 2, z: 4, core: 2. Of those that a mesh axis runs over, the one named last changes fastest.
Arguments:
- queries: bfloat16 [1024, 4096], P('seq', 'tp'), may hold values from -16 to 16
- keyvalues: bfloat16 [2, 1024, 1024], P(None, 'seq', 'tp'), may hold values from -16 to 16
- stretch_order: int32 [8], replicated, may hold values from 0 to 7, each once
- block_table: int32 [8, 8], replicated, may hold values 0 or 1
- proj_weight: bfloat16 [4096, 2048], P('tp'), may hold values from -0.09375 to 0.09375
Outputs:
- projected: bfloat16 [1024, 2048], P('seq', 'tp')
Inputs may be any that keep to these rules, and one draw needn't show every extreme that they name: `stretch_order`: every stretch number 0 to 7 appears once. `block_table`: entry [i, j] matters only where j < i.
All inputs are finite; a program needn't handle non-finite values.
Results may differ from a plain program's by a relative error of at most 0.014.
Values may be sent and summed in bfloat16 or wider, within the bound.
A program may use at most 128 MiB of HBM per device.

v0:
```python
import functools

import jax
import jax.numpy as jnp
from jax import lax
from jax.experimental import pallas as pl
from jax.experimental.pallas import tpu as pltpu
from jax.sharding import PartitionSpec as P

HEAD = 128
MASKED = -1e30
LOG2E = 1.4426950408889634
MESH = pl.DeviceIdType.MESH


def kernel(
    n, tp, q_hbm, kv_hbm, order_hbm, table_hbm, w_hbm, out_ref,
    order, table, q_in, q_rows, k_buf, v_buf, w_buf, run_max, acc, att, parts, got, relay,
    in_sem, k_send, v_send, k_recv, v_recv, k_fwd, v_fwd, p_send, p_recv, r_recv,
):
    rows = q_in.shape[0]
    kv_heads = k_buf.shape[1] // HEAD
    q_heads = q_in.shape[1] // HEAD
    group = q_heads // kv_heads
    grows = group * rows
    width = got.shape[2]
    chips = n // 2
    me = lax.axis_index("seq")
    mt = lax.axis_index("tp")
    chip = me // 2
    core = me % 2
    partner = chip * 2 + 1 - core

    def slot(ref, s, count=1):
        return ref.at[pl.ds(pl.multiple_of(s * rows, rows), count * rows)]

    own_k = pltpu.make_async_copy(kv_hbm.at[0], slot(k_buf, me), in_sem.at[0])
    own_v = pltpu.make_async_copy(kv_hbm.at[1], slot(v_buf, me), in_sem.at[1])
    load_q = pltpu.make_async_copy(q_hbm, q_in, in_sem.at[2])
    load_w = pltpu.make_async_copy(w_hbm, w_buf, in_sem.at[3])
    own_k.start()
    own_v.start()
    load_q.start()
    load_order = pltpu.make_async_copy(order_hbm, order, in_sem.at[4])
    load_table = pltpu.make_async_copy(table_hbm, table, in_sem.at[5])
    load_order.start()
    load_table.start()
    load_w.start()

    barrier = pltpu.get_barrier_semaphore()

    def peer(j):
        return ((chip + j) % chips) * 2 + core

    def each(lo, hi, body):
        if hi - lo <= 8:
            for j in range(lo, hi):
                body(j)
        else:
            lax.fori_loop(lo, hi, lambda j, c: (body(j), c)[1], 0)

    def greet_seq(s):
        pl.semaphore_signal(barrier, inc=1, device_id={"seq": s}, device_id_type=MESH)

    def greet_tp(t):
        pl.semaphore_signal(barrier, inc=1, device_id={"tp": t}, device_id_type=MESH)

    square = chips == 4
    chip_x, chip_y = chip % 2, chip // 2
    xn = (chip_y * 2 + 1 - chip_x) * 2 + 1 - core
    yn = ((1 - chip_y) * 2 + chip_x) * 2 + 1 - core
    dn = ((1 - chip_y) * 2 + 1 - chip_x) * 2 + core
    line = tp == 4
    side = mt // 2
    inner = mt % 2 * (1 - side) + (1 - mt % 2) * side

    def mirror(d):
        return d * (1 - side) + (3 - d) * side

    greet_seq(partner)
    if square:
        greet_seq(xn)
        greet_seq(yn)
        seq_peers = 3
    else:
        each(1, chips, lambda j: greet_seq(peer(j)))
        seq_peers = chips
    if line:
        greet_tp(mirror(2))
        greet_tp(mirror(1 - inner))

        @pl.when(inner == 1)
        def _():
            greet_tp(mirror(3))

        tp_peers = 2 + inner
    else:
        for j in range(1, tp):
            greet_tp((mt + j) % tp)
        tp_peers = tp - 1

    own_k.wait()
    own_v.wait()
    pl.semaphore_wait(barrier, seq_peers + tp_peers)

    def remote(buf, s, send, recv, index, target):
        return pltpu.make_async_remote_copy(
            src_ref=slot(buf, s), dst_ref=slot(buf, s),
            send_sem=send.at[index], recv_sem=recv.at[s],
            device_id={"seq": target}, device_id_type=MESH,
        )

    def send_all(j):
        remote(k_buf, me, k_send, k_recv, j, peer(j)).start()
        remote(v_buf, me, v_send, v_recv, j, peer(j)).start()

    remote(k_buf, me, k_fwd, k_recv, 0, partner).start()
    remote(v_buf, me, v_fwd, v_recv, 0, partner).start()
    if square:
        remote(k_buf, me, k_send, k_recv, 0, xn).start()
        remote(v_buf, me, v_send, v_recv, 0, yn).start()
        remote(v_buf, me, v_send, v_recv, 1, xn).start()
        remote(k_buf, me, k_send, k_recv, 1, yn).start()
    else:
        each(1, chips, send_all)

    load_q.wait()
    for h in range(q_heads):
        q_rows[h * rows:(h + 1) * rows, :] = q_in[:, h * HEAD:(h + 1) * HEAD]

    def bias_of(s):
        key_stretch = order[s]
        seen = jnp.logical_and(key_stretch < my_stretch, table[my_stretch, key_stretch] == 1)
        return jnp.where(seen, 0.0, MASKED).astype(jnp.float32)

    load_order.wait()
    load_table.wait()
    my_stretch = order[me]
    scale = LOG2E / HEAD**0.5

    def attend(slots, first=False):
        count = len(slots)

        def rows_of(buf, cols):
            return jnp.concatenate(
                [buf[pl.ds(pl.multiple_of(s * rows, rows), rows), cols] for s in slots], axis=0
            )

        bias = jnp.concatenate(
            [jnp.full((1, rows), bias_of(s), jnp.float32) for s in slots], axis=1
        )
        for g in range(kv_heads):
            cols = slice(g * HEAD, (g + 1) * HEAD)
            here = slice(g * grows, (g + 1) * grows)
            keys = rows_of(k_buf, cols)
            values = rows_of(v_buf, cols)
            scores = lax.dot_general(
                q_rows[here, :], keys, (((1,), (1,)), ((), ())),
                preferred_element_type=jnp.float32,
            )
            if first:
                shape = (grows, count * rows)
                q_pos = lax.broadcasted_iota(jnp.int32, shape, 0) % rows
                k_pos = lax.broadcasted_iota(jnp.int32, shape, 1)
                scores = jnp.where(
                    k_pos < rows, jnp.where(k_pos <= q_pos, scores, MASKED), scores + bias
                )
            else:
                scores = scores + bias
            top = jnp.max(scores, axis=1, keepdims=True)
            if first:
                new_max = top
            else:
                old_max = run_max[here, 0:1]
                new_max = jnp.maximum(old_max, top)
            weights = jnp.exp2((scores - new_max) * scale).astype(jnp.bfloat16)
            wide = jnp.concatenate([values, jnp.ones_like(values)], axis=1)
            added = jnp.dot(weights, wide, preferred_element_type=jnp.float32)
            if first:
                acc[here, :] = added
            else:
                acc[here, :] = acc[here, :] * jnp.exp2((old_max - new_max) * scale) + added
            run_max[here, :] = jnp.broadcast_to(new_max, (grows, HEAD))

    def wait_slot(s):
        remote(k_buf, s, k_fwd, k_recv, 0, partner).wait_recv()
        remote(v_buf, s, v_fwd, v_recv, 0, partner).wait_recv()

    wait_slot(partner)
    attend([me, partner], True)

    def step(j):
        s = ((chip - j + chips) % chips) * 2 + core
        other = ((chip - j + chips) % chips) * 2 + 1 - core
        remote(k_buf, s, k_fwd, k_recv, j, partner).wait_recv()
        remote(k_buf, s, k_fwd, k_recv, j, partner).start()
        remote(v_buf, s, v_fwd, v_recv, j, partner).wait_recv()
        remote(v_buf, s, v_fwd, v_recv, j, partner).start()
        wait_slot(other)
        attend([s, other])

    def arrive(buf, recv, fwd, s, j, onward=None, send=None):
        remote(buf, s, fwd, recv, j, partner).wait_recv()
        if onward is not None:
            remote(buf, s, send, recv, 2, onward).start()
        remote(buf, s, fwd, recv, j, partner).start()

    if square:
        arrive(k_buf, k_recv, k_fwd, xn, 1, yn, k_send)
        arrive(v_buf, v_recv, v_fwd, yn, 2, xn, v_send)
        arrive(v_buf, v_recv, v_fwd, xn, 1)
        arrive(k_buf, k_recv, k_fwd, yn, 2)
        attend([xn, yn])
        arrive(k_buf, k_recv, k_fwd, dn, 3)
        arrive(v_buf, v_recv, v_fwd, dn, 3)
        xo, yo, do = xn - 1 + 2 * core, yn - 1 + 2 * core, dn + 1 - 2 * core
        wait_slot(xo)
        wait_slot(yo)
        attend([xo, yo, dn])
        wait_slot(do)
        attend([do])
    else:
        each(1, chips, step)

    for h in range(q_heads):
        here = slice(h * rows, (h + 1) * rows)
        att[:, h * HEAD:(h + 1) * HEAD] = (
            acc[here, :HEAD] / acc[here, HEAD:]
        ).astype(jnp.bfloat16)

    load_w.wait()

    def project(t):
        return jnp.dot(
            att[...], w_buf[:, pl.ds(pl.multiple_of(t * width, width), width)],
            preferred_element_type=jnp.float32,
        )

    def part_copy(j, source, target):
        return pltpu.make_async_remote_copy(
            src_ref=parts.at[j], dst_ref=got.at[source],
            send_sem=p_send.at[j], recv_sem=p_recv.at[source],
            device_id={"tp": target}, device_id_type=MESH,
        )

    def piece_copy(i, dst, recv, target):
        piece = pl.ds(i * (rows // 4), rows // 4)
        return pltpu.make_async_remote_copy(
            src_ref=parts.at[2, piece], dst_ref=dst.at[piece],
            send_sem=p_send.at[2 + i], recv_sem=recv,
            device_id={"tp": target}, device_id_type=MESH,
        )

    if line:
        m0, m1, m2, m3 = (mirror(d) for d in range(4))

        @pl.when(inner == 0)
        def _():
            parts[2] = project(m3).astype(jnp.bfloat16)
            for i in range(4):
                piece_copy(i, relay, r_recv.at[i], m1).start()
            parts[0] = project(m2).astype(jnp.bfloat16)
            part_copy(0, mt, m2).start()
            parts[1] = project(m1).astype(jnp.bfloat16)
            part_copy(1, mt, m1).start()
            total = project(mt)
            part_copy(0, m1, m1).wait_recv()
            total = total + got[m1].astype(jnp.float32)
            for i in range(4):
                piece_copy(i, got.at[m2], r_recv.at[i], m2).wait_recv()
            total = total + got[m2].astype(jnp.float32)
            out_ref[...] = total.astype(out_ref.dtype)

        @pl.when(inner == 1)
        def _():
            parts[0] = project(m2).astype(jnp.bfloat16)
            part_copy(0, mt, m2).start()
            parts[1] = project(m0).astype(jnp.bfloat16)
            part_copy(1, mt, m0).start()
            far = project(m3)
            total = project(mt)
            for i in range(4):
                piece = slice(i * (rows // 4), (i + 1) * (rows // 4))
                piece_copy(i, relay, r_recv.at[i], m0).wait_recv()
                parts[2, piece] = (far[piece] + relay[piece].astype(jnp.float32)).astype(jnp.bfloat16)
                piece_copy(i, got.at[mt], r_recv.at[i], m3).start()
            for source in (m2, m3, m0):
                part_copy(0, source, source).wait_recv()
                total = total + got[source].astype(jnp.float32)
            out_ref[...] = total.astype(out_ref.dtype)

        part_copy(0, mt, m2).wait_send()
        part_copy(1, mt, m0).wait_send()
        for i in range(4):
            piece_copy(i, relay, r_recv.at[i], m1).wait_send()
    else:
        ahead = sorted(range(1, tp), key=lambda j: -min(j, tp - j))
        for j in ahead:
            t = (mt + j) % tp
            parts[j] = project(t).astype(jnp.bfloat16)
            part_copy(j, mt, t).start()
        total = project(mt)
        for j in reversed(ahead):
            source = (mt + j) % tp
            part_copy(j, source, source).wait_recv()
            total = total + got[source].astype(jnp.float32)
        out_ref[...] = total.astype(out_ref.dtype)
        for j in ahead:
            part_copy(j, mt, (mt + j) % tp).wait_send()

    def drain(j):
        remote(k_buf, me, k_send, k_recv, j, peer(j)).wait_send()
        remote(v_buf, me, v_send, v_recv, j, peer(j)).wait_send()

    def drain_fwd(j):
        remote(k_buf, me, k_fwd, k_recv, j, partner).wait_send()
        remote(v_buf, me, v_fwd, v_recv, j, partner).wait_send()

    if square:
        for j in range(3):
            remote(k_buf, me, k_send, k_recv, j, yn).wait_send()
            remote(v_buf, me, v_send, v_recv, j, xn).wait_send()
    else:
        each(1, chips, drain)
    each(0, chips, drain_fwd)


def solution(mesh):
    n, tp = mesh.shape["seq"], mesh.shape["tp"]

    def per_device(queries, keyvalues, stretch_order, block_table, proj_weight):
        rows, q_width = queries.shape
        kv_width = keyvalues.shape[2]
        dout = proj_weight.shape[1]
        q_heads = q_width // HEAD
        dma = pltpu.SemaphoreType.DMA
        return pl.pallas_call(
            functools.partial(kernel, n, tp),
            out_shape=jax.ShapeDtypeStruct((rows, dout // tp), jnp.bfloat16),
            in_specs=[
                pl.BlockSpec(memory_space=pl.ANY),
                pl.BlockSpec(memory_space=pl.ANY),
                pl.BlockSpec(memory_space=pl.ANY),
                pl.BlockSpec(memory_space=pl.ANY),
                pl.BlockSpec(memory_space=pl.ANY),
            ],
            out_specs=pl.BlockSpec(memory_space=pltpu.VMEM),
            scratch_shapes=[
                pltpu.SMEM(stretch_order.shape, jnp.int32),
                pltpu.SMEM(block_table.shape, jnp.int32),
                pltpu.VMEM((rows, q_width), jnp.bfloat16),
                pltpu.VMEM((q_heads * rows, HEAD), jnp.bfloat16),
                pltpu.VMEM((n * rows, kv_width), jnp.bfloat16),
                pltpu.VMEM((n * rows, kv_width), jnp.bfloat16),
                pltpu.VMEM(proj_weight.shape, jnp.bfloat16),
                pltpu.VMEM((q_heads * rows, HEAD), jnp.float32),
                pltpu.VMEM((q_heads * rows, 2 * HEAD), jnp.float32),
                pltpu.VMEM((rows, q_width), jnp.bfloat16),
                pltpu.VMEM((tp, rows, dout // tp), jnp.bfloat16),
                pltpu.VMEM((tp, rows, dout // tp), jnp.bfloat16),
                pltpu.VMEM((rows, dout // tp), jnp.bfloat16),
                dma((6,)),
                dma((n // 2,)), dma((n // 2,)),
                dma((n,)), dma((n,)),
                dma((n // 2,)), dma((n // 2,)),
                dma((max(tp, 6),)), dma((tp,)), dma((4,)),
            ],
            compiler_params=pltpu.CompilerParams(
                collective_id=0, has_side_effects=True,
            ),
        )(queries, keyvalues, stretch_order, block_table, proj_weight)

    return jax.shard_map(
        per_device, mesh=mesh,
        in_specs=(P("seq", "tp"), P(None, "seq", "tp"), P(), P(), P("tp", None)),
        out_specs=P("seq", "tp"), check_vma=False,
    )
```

profile of v0, /device:TPU:0, one launch (start us, length us, event | category | flops | bytes accessed | tf_op | source)
XLA Modules:
  0.0 27.5 jit_solution(14394305282401916820)
XLA Ops:
  0.0 26.0 %shard_map.55 = bf16[128,512]{1,0:T(8,128)(2,1)} custom-call(bf16[128,1024]{1,0:T(8,128)(2,1)} %q_hbm.1, bf16[2,128,256]{2,1,0:T(8,128)(2,1)} %kv_hbm.1, s32[8]{0:T(128)} %order_hbm.1, s32[8,8]{1,0:T(8,128)} %table_hbm.1, bf16[1024,2048]{1,0:T(8,128)(2,1)} %w_hbm.1), custom_call_target="tpu_custom_call" | custom-call | tf_op jit(solution)/shard_map/pallas_call | solution.py:337
  26.0 1.6 %copy.7 = bf16[128,512]{1,0:T(8,128)(2,1)} copy(bf16[128,512]{1,0:T(8,128)(2,1)} %shard_map.55) | data formatting | bytes 262144
where the time goes:
time: 27.7 us; the launch traced here: 27.5 us
  Pallas kernels  26 us (94%)
  local copies, waits for them, and re-layouts  1.57 us (6%)
    pallas_call x1, Pallas kernels, per_device(): pl.pallas_call(functools.partial(kernel, n, tp), out_shape=jax.ShapeDtype...  26 us
    unnamed x1, local copies, waits for them, and re-layouts  1.57 us

commit v1 on v0

--- a/solution.py
+++ b/solution.py
@@ -336,7 +336,7 @@
         dma = pltpu.SemaphoreType.DMA
         return pl.pallas_call(
             functools.partial(kernel, n, tp),
-            out_shape=jax.ShapeDtypeStruct((rows, dout // tp), jnp.bfloat16),
+            out_shape=pltpu.VMEM((rows, dout // tp), jnp.bfloat16),
             in_specs=[
                 pl.BlockSpec(memory_space=pl.ANY),
                 pl.BlockSpec(memory_space=pl.ANY),
@@ -366,9 +366,10 @@
                 dma((max(tp, 6),)), dma((tp,)), dma((4,)),
             ],
             compiler_params=pltpu.CompilerParams(
-                collective_id=0, has_side_effects=True,
+                collective_id=0, has_side_effects=True, vmem_limit_bytes=48 << 20,
             ),
-        )(queries, keyvalues, stretch_order, block_table, proj_weight)
+        )(*(pltpu.with_memory_space_constraint(a, pltpu.HBM)
+            for a in (queries, keyvalues, stretch_order, block_table, proj_weight)))
 
     return jax.shard_map(
         per_device, mesh=mesh,

time: 27.7 us -> 26.1 us (0.942)
  local copies, waits for them, and re-layouts: 1.57 us -> 0.66 us
  Pallas kernels: 26 us -> 25.3 us
    unnamed x1, local copies, waits for them, and re-layouts: 1.57 us -> 0.66 us
    pallas_call x1, Pallas kernels: 26 us -> 25.3 us  [per_device(): pl.pallas_call(functools.partial(kernel, n, tp), out_shape=pltpu.VMEM((ro...]
where the time goes in v1:
time: 26.1 us; the launch traced here: 26 us
  Pallas kernels  25.3 us (97%)
  local copies, waits for them, and re-layouts  0.66 us (3%)
    pallas_call x1, Pallas kernels, per_device(): pl.pallas_call(functools.partial(kernel, n, tp), out_shape=pltpu.VMEM((ro...  25.3 us
    unnamed x1, local copies, waits for them, and re-layouts  0.66 us

profile of v1, /device:TPU:0, one launch (start us, length us, event | category | flops | bytes accessed | tf_op | source)
XLA Modules:
  0.0 26.0 jit_solution(3085595119688781457)
XLA Ops:
  0.0 25.3 %shard_map.55 = bf16[128,512]{1,0:T(8,128)(2,1)S(1)} custom-call(bf16[128,1024]{1,0:T(8,128)(2,1)} %q_hbm.1, bf16[2,128,256]{2,1,0:T(8,128)(2,1)} %kv_hbm.1, s32[8]{0:T(128)} %order_hbm.1, s32[8,8]{1,0:T(8,128)} %table_hbm.1, bf16[1024,2048]{1,0:T(8,128)(2,1)} %w_hbm.1), custom_call_target="tpu_custom_call" | custom-call | tf_op jit(solution)/shard_map/pallas_call | solution.py:337
  25.3 0.7 %copy.7 = bf16[128,512]{1,0:T(8,128)(2,1)} copy(bf16[128,512]{1,0:T(8,128)(2,1)S(1)} %shard_map.55) | data formatting | bytes 262144

commit v2 on v1

v2 whole, which is shorter than its diff:
```python
import functools

import jax
import jax.numpy as jnp
from jax import lax
from jax.experimental import pallas as pl
from jax.experimental.pallas import tpu as pltpu
from jax.sharding import PartitionSpec as P

HEAD = 128
MASKED = -1e30
LOG2E = 1.4426950408889634
MESH = pl.DeviceIdType.MESH
F32 = jnp.float32
BF16 = jnp.bfloat16


def kernel(
    n, tp, q_hbm, kv_hbm, order_hbm, table_hbm, w_hbm, out_ref,
    order, table, q_in, q_t, k_buf, v_buf, w_buf, top_ref, acc, den, att, mine, parts, relay, got,
    in_sem, kv_send, k_recv, v_recv, p_send, r_recv, g_recv,
):
    rows = q_in.shape[0]
    kv_heads = k_buf.shape[1]
    q_heads = q_in.shape[1] // HEAD
    group = q_heads // kv_heads
    width = out_ref.shape[1]
    blocks, _, pcols = parts.shape[1:]
    half = rows // 2
    chips = n // 2
    me = lax.axis_index("seq")
    mt = lax.axis_index("tp")
    chip = me // 2
    core = me % 2
    partner = chip * 2 + 1 - core
    heads = range(kv_heads)

    own = []
    for g in heads:
        cols = slice(g * HEAD, (g + 1) * HEAD)
        own.append(pltpu.make_async_copy(kv_hbm.at[0, :, cols], k_buf.at[me, g], in_sem.at[4 + 2 * g]))
        own.append(pltpu.make_async_copy(kv_hbm.at[1, :, cols], v_buf.at[me, g], in_sem.at[5 + 2 * g]))
    load_q = pltpu.make_async_copy(q_hbm, q_in, in_sem.at[0])
    load_w = pltpu.make_async_copy(w_hbm, w_buf, in_sem.at[1])
    load_order = pltpu.make_async_copy(order_hbm, order, in_sem.at[2])
    load_table = pltpu.make_async_copy(table_hbm, table, in_sem.at[3])
    for c in own:
        c.start()
    load_q.start()
    load_order.start()
    load_table.start()
    load_w.start()

    barrier = pltpu.get_barrier_semaphore()

    def peer(j):
        return ((chip + j) % chips) * 2 + core

    def each(lo, hi, body):
        if hi - lo <= 8:
            for j in range(lo, hi):
                body(j)
        else:
            lax.fori_loop(lo, hi, lambda j, c: (body(j), c)[1], 0)

    def greet_seq(s):
        pl.semaphore_signal(barrier, inc=1, device_id={"seq": s}, device_id_type=MESH)

    def greet_tp(t):
        pl.semaphore_signal(barrier, inc=1, device_id={"tp": t}, device_id_type=MESH)

    square = chips == 4
    chip_x, chip_y = chip % 2, chip // 2
    x0 = (chip_y * 2 + 1 - chip_x) * 2
    y0 = ((1 - chip_y) * 2 + chip_x) * 2
    d0 = ((1 - chip_y) * 2 + 1 - chip_x) * 2
    x1, y1, d1 = x0 + 1, y0 + 1, d0 + 1
    line = tp == 4
    side = mt // 2
    inner = mt % 2 * (1 - side) + (1 - mt % 2) * side

    def mirror(d):
        return d * (1 - side) + (3 - d) * side

    greet_seq(partner)
    if square:
        greet_seq(x1)
        greet_seq(y1)

        @pl.when(core == 1)
        def _():
            greet_seq(x0)
            greet_seq(y0)

        seq_peers = 3 + 2 * core
    else:
        each(1, chips, lambda j: greet_seq(peer(j)))
        seq_peers = chips
    if line:
        greet_tp(mirror(2))
        greet_tp(mirror(1 - inner))

        @pl.when(inner == 1)
        def _():
            greet_tp(mirror(3))

        tp_peers = 2 + inner
    else:
        for j in range(1, tp):
            greet_tp((mt + j) % tp)
        tp_peers = tp - 1

    for c in own:
        c.wait()
    pl.semaphore_wait(barrier, seq_peers + tp_peers)

    def piece(buf, recv, s, g, index, target):
        return pltpu.make_async_remote_copy(
            src_ref=buf.at[s, g], dst_ref=buf.at[s, g],
            send_sem=kv_send.at[index], recv_sem=recv.at[s, g],
            device_id={"seq": target}, device_id_type=MESH,
        )

    def k_piece(s, g, index, target):
        return piece(k_buf, k_recv, s, g, index, target)

    def v_piece(s, g, index, target):
        return piece(v_buf, v_recv, s, g, index, target)

    base = 4 * kv_heads
    mark = 2 * kv_heads
    if square:
        for g in heads:
            k_piece(me, g, g, x1).start()
            v_piece(me, g, mark + g, y1).start()
            k_piece(me, g, base + g, partner).start()
            v_piece(me, g, base + kv_heads + g, partner).start()
        for g in heads:
            v_piece(me, g, kv_heads + g, x1).start()
            k_piece(me, g, mark + kv_heads + g, y1).start()
        base += mark
    else:
        def send_all(j, target):
            for g in heads:
                k_piece(me, g, j * mark + g, target).start()
                v_piece(me, g, j * mark + kv_heads + g, target).start()

        send_all(0, partner)
        each(1, chips, lambda j: send_all(j, peer(j)))
        base = mark * chips

    load_q.wait()
    for g in heads:
        for j in range(group):
            h = g * group + j
            q_t[g, :, j * rows:(j + 1) * rows] = q_in[:, h * HEAD:(h + 1) * HEAD].T

    load_order.wait()
    load_table.wait()
    my_stretch = order[me]
    scale = LOG2E / HEAD**0.5

    def bias_of(s):
        key_stretch = order[s]
        seen = jnp.logical_and(key_stretch < my_stretch, table[my_stretch, key_stretch] == 1)
        return jnp.where(seen, 0.0, MASKED).astype(F32)

    def attend(g, slots, first=False):
        queries = q_t[g]
        scores, tops, biases = [], [], []
        for i, s in enumerate(slots):
            part = jnp.dot(k_buf[s, g], queries, preferred_element_type=F32)
            if first and i == 0:
                k_pos = lax.broadcasted_iota(jnp.int32, part.shape, 0)
                q_pos = lax.broadcasted_iota(jnp.int32, part.shape, 1) % rows
                part = jnp.where(k_pos <= q_pos, part, MASKED)
                bias = 0.0
            else:
                bias = bias_of(s)
            scores.append(part)
            biases.append(bias)
            tops.append(jnp.max(part, axis=0, keepdims=True) + bias)
        new_top = functools.reduce(jnp.maximum, tops)
        if not first:
            old_top = top_ref[g]
            new_top = jnp.maximum(new_top, old_top)
        weights = jnp.concatenate(
            [jnp.exp2((p - (new_top - b)) * scale).astype(BF16) for p, b in zip(scores, biases)], axis=0
        )
        values = jnp.concatenate([v_buf[s, g] for s in slots], axis=0).T
        tall = jnp.concatenate([values, jnp.ones((16, values.shape[1]), BF16)], axis=0)
        added = jnp.dot(tall, weights, preferred_element_type=F32)
        if first:
            acc[g] = added[:HEAD]
            den[g] = added[HEAD:HEAD + 8]
        else:
            fade = jnp.exp2((old_top - new_top) * scale)
            acc[g] = acc[g] * fade + added[:HEAD]
            den[g] = den[g] * fade + added[HEAD:HEAD + 8]
        top_ref[g] = new_top

    def wait_slot(s, g):
        k_piece(s, g, 0, partner).wait_recv()
        v_piece(s, g, 0, partner).wait_recv()

    for g in heads:
        wait_slot(partner, g)
    for g in heads:
        attend(g, [me, partner], True)

    if square:
        near = [x1, y1, x0, y0]

        def hand_on(make, s, g, index, target=None, mark=0):
            make(s, g, 0, partner).wait_recv()
            if target is not None:
                make(s, g, mark, target).start()
            make(s, g, index, partner).start()

        relays = base
        hops = base + 4 * kv_heads

        @pl.when(core == 1)
        def _():
            i = 0
            for g in heads:
                for sx, sy in ((x1, y1), (x0, y0)):
                    hand_on(k_piece, sx, g, hops + i, y0, relays + i)
                    hand_on(v_piece, sy, g, hops + i + 1, x0, relays + i + 1)
                    i += 2

        for g in heads:
            @pl.when(core == 1)
            def _(g=g):
                i = hops + (kv_heads + g) * 4
                for sx, sy in ((x1, y1), (x0, y0)):
                    hand_on(v_piece, sx, g, i)
                    hand_on(k_piece, sy, g, i + 1)
                    i += 2

            @pl.when(core == 0)
            def _(g=g):
                for s in near:
                    wait_slot(s, g)

            attend(g, near)

            @pl.when(core == 0)
            def _(g=g):
                i = relays + g * 4
                for s in (d1, d0):
                    hand_on(k_piece, s, g, i)
                    hand_on(v_piece, s, g, i + 1)
                    i += 2

        for g in heads:
            @pl.when(core == 1)
            def _(g=g):
                wait_slot(d1, g)
                wait_slot(d0, g)

            attend(g, [d1, d0])
    else:
        def step(j):
            s = ((chip - j + chips) % chips) * 2 + core
            other = ((chip - j + chips) % chips) * 2 + 1 - core
            for g in heads:
                k_piece(s, g, 0, partner).wait_recv()
                k_piece(s, g, base + (j - 1) * mark + g, partner).start()
                v_piece(s, g, 0, partner).wait_recv()
                v_piece(s, g, base + (j - 1) * mark + kv_heads + g, partner).start()
            for g in heads:
                wait_slot(other, g)
            for g in heads:
                attend(g, [s, other])

        each(1, chips, step)

    for g in heads:
        share = 1.0 / den[g][0:1]
        for j in range(group):
            h = g * group + j
            cols = slice(j * rows, (j + 1) * rows)
            att[:, h * HEAD:(h + 1) * HEAD] = (acc[g, :, cols] * share[:, cols]).astype(BF16).T

    load_w.wait()

    def project(t, b):
        cols = pl.ds(pl.multiple_of(t * width + b * pcols, pcols), pcols)
        return jnp.dot(att[...], w_buf[:, cols], preferred_element_type=F32)

    def part_of(ref, slot, i):
        return ref.at[slot, i // 2, pl.ds(i % 2 * half, half)]

    def send_part(c, i, dst, slot, recv, target):
        return pltpu.make_async_remote_copy(
            src_ref=part_of(parts, c, i), dst_ref=part_of(dst, slot, i),
            send_sem=p_send.at[c, i], recv_sem=recv.at[slot, i],
            device_id={"tp": target}, device_id_type=MESH,
        )

    pieces = 2 * blocks
    if line:
        m0, m1, m2, m3 = (mirror(d) for d in range(4))

        def send_product(c, t, dst, slot, recv, target):
            for b in range(blocks):
                parts[c, b] = project(t, b).astype(BF16)
                for i in (2 * b, 2 * b + 1):
                    send_part(c, i, dst, slot, recv, target).start()

        @pl.when(inner == 0)
        def _():
            send_product(0, m3, relay, 0, r_recv, m1)
            send_product(1, m2, relay, 1, r_recv, m1)
            send_product(2, m1, got, 0, g_recv, m1)
            for b in range(blocks):
                mine[0, b] = project(mt, b)

        @pl.when(inner == 1)
        def _():
            send_product(2, m0, got, 0, g_recv, m0)
            for c, t in ((1, m3), (2, m2), (0, mt)):
                for b in range(blocks):
                    mine[c, b] = project(t, b)
            for c, target in ((0, m3), (1, m2)):
                for i in range(pieces):
                    b, r = i // 2, slice(i % 2 * half, (i % 2 + 1) * half)
                    send_part(2, i, relay, c, r_recv, m0).wait_recv()
                    parts[c, b, r] = (mine[1 + c, b, r] + relay[c, b, r].astype(F32)).astype(BF16)
                    send_part(c, i, got, 1, g_recv, target).start()

        for i in range(pieces):
            send_part(2, i, got, 0, g_recv, m0).wait_recv()
        for b in range(blocks):
            mine[0, b] = mine[0, b] + got[0, b].astype(F32)
        for i in range(pieces):
            b, r = i // 2, slice(i % 2 * half, (i % 2 + 1) * half)
            send_part(2, i, got, 1, g_recv, m0).wait_recv()
            out_ref[r, b * pcols:(b + 1) * pcols] = (mine[0, b, r] + got[1, b, r].astype(F32)).astype(BF16)
        for c in range(3):
            for i in range(pieces):
                send_part(c, i, got, 0, g_recv, m0).wait_send()
    else:
        ahead = sorted(range(1, tp), key=lambda j: -min(j, tp - j))
        for j in ahead:
            t = (mt + j) % tp
            for b in range(blocks):
                parts[j, b] = project(t, b).astype(BF16)
                for i in (2 * b, 2 * b + 1):
                    send_part(j, i, got, mt, g_recv, t).start()
        for b in range(blocks):
            mine[0, b] = project(mt, b)
        for j in reversed(ahead):
            source = (mt + j) % tp
            for i in range(pieces):
                send_part(j, i, got, source, g_recv, source).wait_recv()
            for b in range(blocks):
                mine[0, b] = mine[0, b] + got[source, b].astype(F32)
        for b in range(blocks):
            out_ref[:, b * pcols:(b + 1) * pcols] = mine[0, b].astype(BF16)
        for j in ahead:
            for i in range(pieces):
                send_part(j, i, got, mt, g_recv, mt).wait_send()

    def drain(i):
        k_piece(me, 0, i, partner).wait_send()

    if square:
        each(0, base, drain)
        each(base, base + 4 * kv_heads, drain)

        @pl.when(core == 1)
        def _():
            each(base + 4 * kv_heads, base + 12 * kv_heads, drain)
    else:
        each(0, 2 * base - mark, drain)


def solution(mesh):
    n, tp = mesh.shape["seq"], mesh.shape["tp"]

    def per_device(queries, keyvalues, stretch_order, block_table, proj_weight):
        rows, q_width = queries.shape
        kv_heads = keyvalues.shape[2] // HEAD
        width = proj_weight.shape[1] // tp
        pcols = 2 * HEAD if width % (2 * HEAD) == 0 else HEAD
        blocks = width // pcols
        group_rows = q_width // HEAD // kv_heads * rows
        line = tp == 4
        n_parts, n_got, n_mine = (3, 2, 3) if line else (tp, tp, 1)
        n_sends = 18 * kv_heads if n == 8 else 2 * kv_heads * n
        dma = pltpu.SemaphoreType.DMA
        args = (queries, keyvalues, stretch_order, block_table, proj_weight)
        return pl.pallas_call(
            functools.partial(kernel, n, tp),
            out_shape=pltpu.VMEM((rows, width), BF16),
            in_specs=[pl.BlockSpec(memory_space=pltpu.HBM)] * 5,
            out_specs=pl.BlockSpec(memory_space=pltpu.VMEM),
            scratch_shapes=[
                pltpu.SMEM(stretch_order.shape, jnp.int32),
                pltpu.SMEM(block_table.shape, jnp.int32),
                pltpu.VMEM((rows, q_width), BF16),
                pltpu.VMEM((kv_heads, HEAD, group_rows), BF16),
                pltpu.VMEM((n, kv_heads, rows, HEAD), BF16),
                pltpu.VMEM((n, kv_heads, rows, HEAD), BF16),
                pltpu.VMEM(proj_weight.shape, BF16),
                pltpu.VMEM((kv_heads, 1, group_rows), F32),
                pltpu.VMEM((kv_heads, HEAD, group_rows), F32),
                pltpu.VMEM((kv_heads, 8, group_rows), F32),
                pltpu.VMEM((rows, q_width), BF16),
                pltpu.VMEM((n_mine, blocks, rows, pcols), F32),
                pltpu.VMEM((n_parts, blocks, rows, pcols), BF16),
                pltpu.VMEM((2, blocks, rows, pcols), BF16),
                pltpu.VMEM((n_got, blocks, rows, pcols), BF16),
                dma((4 + 2 * kv_heads,)),
                dma((n_sends,)),
                dma((n, kv_heads)), dma((n, kv_heads)),
                dma((n_parts, 2 * blocks)), dma((2, 2 * blocks)), dma((n_got, 2 * blocks)),
            ],
            compiler_params=pltpu.CompilerParams(
                collective_id=0, has_side_effects=True, vmem_limit_bytes=48 << 20,
            ),
        )(*(pltpu.with_memory_space_constraint(a, pltpu.HBM) for a in args))

    return jax.shard_map(
        per_device, mesh=mesh,
        in_specs=(P("seq", "tp"), P(None, "seq", "tp"), P(), P(), P("tp", None)),
        out_specs=P("seq", "tp"), check_vma=False,
    )
```

time: 26.1 us -> 23.9 us (0.916)
  the two profiles are of different devices: /device:TPU:0 before, /device:TPU:9 now
where the time goes in v2:
time: 23.9 us; the launch traced here: 23.7 us
  Pallas kernels  23 us (96%)
  local copies, waits for them, and re-layouts  0.66 us (3%)
    pallas_call x1, Pallas kernels, per_device(): pl.pallas_call(functools.partial(kernel, n, tp), out_shape=pltpu.VMEM((ro...  23 us
    unnamed x1, local copies, waits for them, and re-layouts  0.66 us

profile of v2, /device:TPU:9, one launch (start us, length us, event | category | flops | bytes accessed | tf_op | source)
XLA Modules:
  0.0 23.7 jit_solution(15979873859630205572)
XLA Ops:
  0.0 23.0 %shard_map.55 = bf16[128,512]{1,0:T(8,128)(2,1)S(1)} custom-call(bf16[128,1024]{1,0:T(8,128)(2,1)} %q_hbm.1, bf16[2,128,256]{2,1,0:T(8,128)(2,1)} %kv_hbm.1, s32[8]{0:T(128)} %order_hbm.1, s32[8,8]{1,0:T(8,128)} %table_hbm.1, bf16[1024,2048]{1,0:T(8,128)(2,1)} %w_hbm.1), custom_call_target="tpu_custom_call" | custom-call | tf_op jit(solution)/shard_map/pallas_call | solution.py:395
  23.1 0.7 %copy.7 = bf16[128,512]{1,0:T(8,128)(2,1)} copy(bf16[128,512]{1,0:T(8,128)(2,1)S(1)} %shard_map.55) | data formatting | bytes 262144

commit v3 on v2

v3 whole, which is shorter than its diff:
```python
import functools

import jax
import jax.numpy as jnp
from jax import lax
from jax.experimental import pallas as pl
from jax.experimental.pallas import tpu as pltpu
from jax.sharding import PartitionSpec as P

HEAD = 128
MASKED = -1e30
LOG2E = 1.4426950408889634
MESH = pl.DeviceIdType.MESH
F32 = jnp.float32
BF16 = jnp.bfloat16


def kernel(
    n, tp, q_hbm, kv_hbm, order_hbm, table_hbm, w_hbm, out_ref,
    order, table, q_in, q_t, kv_buf, w_buf, top_ref, acc, den, att, mine, parts, relay, got,
    in_sem, kv_send, kv_recv, hop_recv, p_send, r_recv, g_recv, f_recv,
):
    rows = q_in.shape[0]
    kv_heads = kv_buf.shape[1]
    q_heads = q_in.shape[1] // HEAD
    group = q_heads // kv_heads
    width = out_ref.shape[1]
    blocks, _, pcols = parts.shape[1:]
    half = rows // 2
    chips = n // 2
    me = lax.axis_index("seq")
    mt = lax.axis_index("tp")
    chip = me // 2
    core = me % 2
    partner = chip * 2 + 1 - core
    heads = range(kv_heads)

    own = [
        pltpu.make_async_copy(
            kv_hbm.at[i, :, slice(g * HEAD, (g + 1) * HEAD)], kv_buf.at[me, g, i], in_sem.at[4]
        )
        for g in heads for i in range(2)
    ]
    load_q = pltpu.make_async_copy(q_hbm, q_in, in_sem.at[0])
    load_w = pltpu.make_async_copy(w_hbm, w_buf, in_sem.at[1])
    load_order = pltpu.make_async_copy(order_hbm, order, in_sem.at[2])
    load_table = pltpu.make_async_copy(table_hbm, table, in_sem.at[3])
    for c in own:
        c.start()
    load_q.start()
    load_order.start()
    load_table.start()
    load_w.start()

    barrier = pltpu.get_barrier_semaphore()

    def peer(j):
        return ((chip + j) % chips) * 2 + core

    def each(lo, hi, body):
        if hi - lo <= 8:
            for j in range(lo, hi):
                body(j)
        else:
            lax.fori_loop(lo, hi, lambda j, c: (body(j), c)[1], 0)

    def greet_seq(s):
        pl.semaphore_signal(barrier, inc=1, device_id={"seq": s}, device_id_type=MESH)

    def greet_tp(t):
        pl.semaphore_signal(barrier, inc=1, device_id={"tp": t}, device_id_type=MESH)

    square = chips == 4
    chip_x, chip_y = chip % 2, chip // 2
    x0 = (chip_y * 2 + 1 - chip_x) * 2
    y0 = ((1 - chip_y) * 2 + chip_x) * 2
    d0 = ((1 - chip_y) * 2 + 1 - chip_x) * 2
    x1, y1, d1 = x0 + 1, y0 + 1, d0 + 1
    line = tp == 4
    side = mt // 2
    inner = mt % 2 * (1 - side) + (1 - mt % 2) * side

    def mirror(d):
        return d * (1 - side) + (3 - d) * side

    greet_seq(partner)
    if square:
        greet_seq(x1)
        greet_seq(y1)

        @pl.when(core == 1)
        def _():
            greet_seq(x0)
            greet_seq(y0)

        seq_peers = 3 + 2 * core
    else:
        each(1, chips, lambda j: greet_seq(peer(j)))
        seq_peers = chips
    if line:
        greet_tp(mirror(2))
        greet_tp(mirror(1 - inner))

        @pl.when(inner == 1)
        def _():
            greet_tp(mirror(3))

        tp_peers = 2 + inner
    else:
        for j in range(1, tp):
            greet_tp((mt + j) % tp)
        tp_peers = tp - 1

    pltpu.make_async_copy(kv_buf.at[me], kv_buf.at[me], in_sem.at[4]).wait()
    pl.semaphore_wait(barrier, seq_peers + tp_peers)

    def copy(ref, recv_sem, target, turn=0):
        return pltpu.make_async_remote_copy(
            src_ref=ref, dst_ref=ref, send_sem=kv_send.at[turn], recv_sem=recv_sem,
            device_id={"seq": target}, device_id_type=MESH,
        )

    def slot(s, target):
        return copy(kv_buf.at[s], kv_recv.at[s], target)

    def near_sem(axis, c, g, i):
        return kv_recv.at[((axis * 2 + c) * kv_heads + g) * 2 + i]

    def far_sem(c, g, i):
        return kv_recv.at[(c * kv_heads + g) * 2 + i]

    def several(slots, recv_sem, turn=0):
        return copy(kv_buf.at[pl.ds(0, slots)], recv_sem, partner, turn)

    if square:
        for g in heads:
            for i in range(2):
                copy(kv_buf.at[me, g, i], hop_recv.at[0], partner).start()
        for i in range(2):
            for g in heads:
                copy(kv_buf.at[me, g, i], near_sem(0, core, g, i), x1).start()
                copy(kv_buf.at[me, g, 1 - i], near_sem(1, core, g, 1 - i), y1).start()
    else:
        slot(me, partner).start()
        each(1, chips, lambda j: slot(me, peer(j)).start())

    load_q.wait()
    for g in heads:
        for j in range(group):
            h = g * group + j
            q_t[g, :, j * rows:(j + 1) * rows] = q_in[:, h * HEAD:(h + 1) * HEAD].T

    load_order.wait()
    load_table.wait()
    my_stretch = order[me]
    scale = LOG2E / HEAD**0.5

    def bias_of(s):
        key_stretch = order[s]
        seen = jnp.logical_and(key_stretch < my_stretch, table[my_stretch, key_stretch] == 1)
        return jnp.where(seen, 0.0, MASKED).astype(F32)

    def attend(g, slots, first=False):
        queries = q_t[g]
        scores, tops, biases = [], [], []
        for i, s in enumerate(slots):
            part = jnp.dot(kv_buf[s, g, 0], queries, preferred_element_type=F32)
            if first and i == 0:
                k_pos = lax.broadcasted_iota(jnp.int32, part.shape, 0)
                q_pos = lax.broadcasted_iota(jnp.int32, part.shape, 1) % rows
                part = jnp.where(k_pos <= q_pos, part, MASKED)
                bias = 0.0
            else:
                bias = bias_of(s)
            scores.append(part)
            biases.append(bias)
            tops.append(jnp.max(part, axis=0, keepdims=True) + bias)
        new_top = functools.reduce(jnp.maximum, tops)
        if not first:
            old_top = top_ref[g]
            new_top = jnp.maximum(new_top, old_top)
        weights = jnp.concatenate(
            [jnp.exp2((p - (new_top - b)) * scale).astype(BF16) for p, b in zip(scores, biases)], axis=0
        )
        values = jnp.concatenate([kv_buf[s, g, 1] for s in slots], axis=0).T
        tall = jnp.concatenate([values, jnp.ones((16, values.shape[1]), BF16)], axis=0)
        added = jnp.dot(tall, weights, preferred_element_type=F32)
        if first:
            acc[g] = added[:HEAD]
            den[g] = added[HEAD:HEAD + 8]
        else:
            fade = jnp.exp2((old_top - new_top) * scale)
            acc[g] = acc[g] * fade + added[:HEAD]
            den[g] = den[g] * fade + added[HEAD:HEAD + 8]
        top_ref[g] = new_top

    if square:
        several(1, hop_recv.at[0]).wait_recv()
    else:
        slot(partner, partner).wait_recv()
    for g in heads:
        attend(g, [me, partner], True)

    if square:
        near, far = [x1, y1, x0, y0], [d1, d0]

        def arrive(s, g, i, sem, onward=None, onward_sem=None):
            ref = kv_buf.at[s, g, i]
            copy(ref, sem, partner).wait_recv()
            if onward is not None:
                copy(ref, onward_sem, onward, 1).start()
            copy(ref, hop_recv.at[1 + g], partner, 1).start()

        @pl.when(core == 1)
        def _():
            for g in heads:
                for c, sx, sy in ((1, x1, y1), (0, x0, y0)):
                    arrive(sx, g, 0, near_sem(0, c, g, 0), y0, far_sem(c, g, 0))
                    arrive(sy, g, 1, near_sem(1, c, g, 1), x0, far_sem(c, g, 1))
            for g in heads:
                for c, sx, sy in ((1, x1, y1), (0, x0, y0)):
                    arrive(sx, g, 1, near_sem(0, c, g, 1))
                    arrive(sy, g, 0, near_sem(1, c, g, 0))
                attend(g, near)
            for g in heads:
                several(1, hop_recv.at[1 + g]).wait_recv()
                attend(g, far)

        @pl.when(core == 0)
        def _():
            for g in heads:
                several(2, hop_recv.at[1 + g]).wait_recv()
                last = g == kv_heads - 1
                if not last:
                    attend(g, near)
                for c, s in ((1, d1), (0, d0)):
                    for i in range(2):
                        arrive(s, g, i, far_sem(c, g, i))
                attend(g, near + far if last else far)
    else:
        def step(j):
            s = ((chip - j + chips) % chips) * 2 + core
            other = ((chip - j + chips) % chips) * 2 + 1 - core
            slot(s, partner).wait_recv()
            slot(s, partner).start()
            slot(other, partner).wait_recv()
            for g in heads:
                attend(g, [s, other])

        each(1, chips, step)

    for g in heads:
        share = 1.0 / den[g][0:1]
        for j in range(group):
            h = g * group + j
            cols = slice(j * rows, (j + 1) * rows)
            att[:, h * HEAD:(h + 1) * HEAD] = (acc[g, :, cols] * share[:, cols]).astype(BF16).T

    load_w.wait()

    def project(t, b):
        cols = pl.ds(pl.multiple_of(t * width + b * pcols, pcols), pcols)
        return jnp.dot(att[...], w_buf[:, cols], preferred_element_type=F32)

    def part_of(ref, slot, i):
        return ref.at[slot, i // 2, pl.ds(i % 2 * half, half)]

    def send_part(c, i, dst, slot, recv_sem, target):
        return pltpu.make_async_remote_copy(
            src_ref=part_of(parts, c, i), dst_ref=part_of(dst, slot, i),
            send_sem=p_send.at[c], recv_sem=recv_sem,
            device_id={"tp": target}, device_id_type=MESH,
        )

    def whole_part(c, slot):
        return pltpu.make_async_remote_copy(
            src_ref=parts.at[c], dst_ref=got.at[slot], send_sem=p_send.at[c], recv_sem=g_recv.at[slot],
            device_id={"tp": mt}, device_id_type=MESH,
        )

    def drain():
        if square:
            several(3, hop_recv.at[0]).wait_send()

            @pl.when(core == 1)
            def _():
                several(6, hop_recv.at[0], 1).wait_send()

            @pl.when(core == 0)
            def _():
                several(2, hop_recv.at[0], 1).wait_send()
        else:
            several(n - 1, hop_recv.at[0]).wait_send()

    pieces = 2 * blocks
    if line:
        m0, m1, m2, m3 = (mirror(d) for d in range(4))

        def send_product(c, t, dst, slot, recv_sems, target):
            for b in range(blocks):
                parts[c, b] = project(t, b).astype(BF16)
                for i in (2 * b, 2 * b + 1):
                    send_part(c, i, dst, slot, recv_sems(i), target).start()

        def keep_own():
            for b in range(blocks):
                mine[0, b] = project(mt, b)

        @pl.when(inner == 0)
        def _():
            send_product(0, m3, relay, 0, lambda i: r_recv.at[0, i], m1)
            send_product(1, m2, relay, 1, lambda i: r_recv.at[1, i], m1)
            send_product(2, m1, got, 0, lambda i: g_recv.at[0], m1)
            keep_own()

        @pl.when(inner == 1)
        def _():
            send_product(2, m0, got, 0, lambda i: g_recv.at[0], m0)
            for c, t in ((1, m3), (2, m2), (0, mt)):
                for b in range(blocks):
                    mine[c, b] = project(t, b)
            for c, target in ((0, m3), (1, m2)):
                for i in range(pieces):
                    b, r = i // 2, slice(i % 2 * half, (i % 2 + 1) * half)
                    send_part(2, i, relay, c, r_recv.at[c, i], m0).wait_recv()
                    parts[c, b, r] = (mine[1 + c, b, r] + relay[c, b, r].astype(F32)).astype(BF16)
                    send_part(c, i, got, 1, f_recv.at[i], target).start()

        drain()
        whole_part(0, 0).wait_send()
        whole_part(2, 0).wait_recv()
        for b in range(blocks):
            mine[0, b] = mine[0, b] + got[0, b].astype(F32)
        whole_part(1 + inner, 0).wait_send()
        for i in range(pieces):
            b, r = i // 2, slice(i % 2 * half, (i % 2 + 1) * half)
            send_part(2, i, got, 1, f_recv.at[i], m0).wait_recv()
            out_ref[r, b * pcols:(b + 1) * pcols] = (mine[0, b, r] + got[1, b, r].astype(F32)).astype(BF16)
        whole_part(2 - inner, 0).wait_send()
    else:
        ahead = sorted(range(1, tp), key=lambda j: -min(j, tp - j))
        for j in ahead:
            t = (mt + j) % tp
            for b in range(blocks):
                parts[j, b] = project(t, b).astype(BF16)
                for i in (2 * b, 2 * b + 1):
                    send_part(j, i, got, mt, g_recv.at[mt], t).start()
        for b in range(blocks):
            mine[0, b] = project(mt, b)
        drain()
        for j in reversed(ahead):
            source = (mt + j) % tp
            whole_part(j, source).wait_recv()
            for b in range(blocks):
                mine[0, b] = mine[0, b] + got[source, b].astype(F32)
        for b in range(blocks):
            out_ref[:, b * pcols:(b + 1) * pcols] = mine[0, b].astype(BF16)
        for j in ahead:
            whole_part(j, 0).wait_send()


def solution(mesh):
    n, tp = mesh.shape["seq"], mesh.shape["tp"]

    def per_device(queries, keyvalues, stretch_order, block_table, proj_weight):
        rows, q_width = queries.shape
        kv_heads = keyvalues.shape[2] // HEAD
        width = proj_weight.shape[1] // tp
        pcols = 2 * HEAD if width % (2 * HEAD) == 0 else HEAD
        blocks = width // pcols
        group_rows = q_width // HEAD // kv_heads * rows
        line = tp == 4
        n_parts, n_got, n_mine = (3, 2, 3) if line else (tp, tp, 1)
        dma = pltpu.SemaphoreType.DMA
        args = (queries, keyvalues, stretch_order, block_table, proj_weight)
        return pl.pallas_call(
            functools.partial(kernel, n, tp),
            out_shape=pltpu.VMEM((rows, width), BF16),
            in_specs=[pl.BlockSpec(memory_space=pltpu.HBM)] * 5,
            out_specs=pl.BlockSpec(memory_space=pltpu.VMEM),
            scratch_shapes=[
                pltpu.SMEM(stretch_order.shape, jnp.int32),
                pltpu.SMEM(block_table.shape, jnp.int32),
                pltpu.VMEM((rows, q_width), BF16),
                pltpu.VMEM((kv_heads, HEAD, group_rows), BF16),
                pltpu.VMEM((n, kv_heads, 2, rows, HEAD), BF16),
                pltpu.VMEM(proj_weight.shape, BF16),
                pltpu.VMEM((kv_heads, 1, group_rows), F32),
                pltpu.VMEM((kv_heads, HEAD, group_rows), F32),
                pltpu.VMEM((kv_heads, 8, group_rows), F32),
                pltpu.VMEM((rows, q_width), BF16),
                pltpu.VMEM((n_mine, blocks, rows, pcols), F32),
                pltpu.VMEM((n_parts, blocks, rows, pcols), BF16),
                pltpu.VMEM((2, blocks, rows, pcols), BF16),
                pltpu.VMEM((n_got, blocks, rows, pcols), BF16),
                dma((5,)), dma((2,)), dma((max(n, 8 * kv_heads) if n == 8 else n,)), dma((1 + kv_heads,)),
                dma((n_parts,)), dma((2, 2 * blocks)), dma((n_got,)), dma((2 * blocks,)),
            ],
            compiler_params=pltpu.CompilerParams(
                collective_id=0, has_side_effects=True, vmem_limit_bytes=48 << 20,
            ),
        )(*(pltpu.with_memory_space_constraint(a, pltpu.HBM) for a in args))

    return jax.shard_map(
        per_device, mesh=mesh,
        in_specs=(P("seq", "tp"), P(None, "seq", "tp"), P(), P(), P("tp", None)),
        out_specs=P("seq", "tp"), check_vma=False,
    )
```

time: 23.9 us -> 23 us (0.962)
  Pallas kernels: 23 us -> 22.2 us
    pallas_call x1, Pallas kernels: 23 us -> 22.2 us  [per_device(): pl.pallas_call(functools.partial(kernel, n, tp), out_shape=pltpu.VMEM((ro...]
where the time goes in v3:
time: 23 us; the launch traced here: 22.9 us
  Pallas kernels  22.2 us (97%)
  local copies, waits for them, and re-layouts  0.66 us (3%)
    pallas_call x1, Pallas kernels, per_device(): pl.pallas_call(functools.partial(kernel, n, tp), out_shape=pltpu.VMEM((ro...  22.2 us
    unnamed x1, local copies, waits for them, and re-layouts  0.66 us

profile of v3, /device:TPU:9, one launch (start us, length us, event | category | flops | bytes accessed | tf_op | source)
XLA Modules:
  0.0 22.9 jit_solution(8452678573299390618)
XLA Ops:
  0.0 22.2 %shard_map.55 = bf16[128,512]{1,0:T(8,128)(2,1)S(1)} custom-call(bf16[128,1024]{1,0:T(8,128)(2,1)} %q_hbm.1, bf16[2,128,256]{2,1,0:T(8,128)(2,1)} %kv_hbm.1, s32[8]{0:T(128)} %order_hbm.1, s32[8,8]{1,0:T(8,128)} %table_hbm.1, bf16[1024,2048]{1,0:T(8,128)(2,1)} %w_hbm.1), custom_call_target="tpu_custom_call" | custom-call | tf_op jit(solution)/shard_map/pallas_call | solution.py:376
  22.2 0.7 %copy.7 = bf16[128,512]{1,0:T(8,128)(2,1)} copy(bf16[128,512]{1,0:T(8,128)(2,1)S(1)} %shard_map.55) | data formatting | bytes 262144

commit v4 on v3

--- a/solution.py
+++ b/solution.py
@@ -18,7 +18,7 @@
 def kernel(
     n, tp, q_hbm, kv_hbm, order_hbm, table_hbm, w_hbm, out_ref,
     order, table, q_in, q_t, kv_buf, w_buf, top_ref, acc, den, att, mine, parts, relay, got,
-    in_sem, kv_send, kv_recv, hop_recv, p_send, r_recv, g_recv, f_recv,
+    in_sem, kv_send, kv_recv, hop_recv, p_send, r_recv, g_recv, f_recv, go,
 ):
     rows = q_in.shape[0]
     kv_heads = kv_buf.shape[1]
@@ -83,36 +83,60 @@
     def mirror(d):
         return d * (1 - side) + (3 - d) * side
 
-    greet_seq(partner)
-    if square:
-        greet_seq(x1)
-        greet_seq(y1)
+    def entered(t):
+        pl.semaphore_signal(barrier, inc=1, device_id={"seq": chip * 2, "tp": t}, device_id_type=MESH)
+
+    split = square and line
+    if split:
+        @pl.when(core == 0)
+        def _():
+            greet_seq(partner)
+
+        greet_seq(x0 + core)
+        greet_seq(y0 + core)
+        entered(mirror(2))
+        entered(mirror(1 - inner))
+
+        @pl.when(inner == 1)
+        def _():
+            entered(mirror(3))
+
+        def tell_partner():
+            pl.semaphore_signal(go, inc=1, device_id={"seq": partner}, device_id_type=MESH)
 
         @pl.when(core == 1)
         def _():
-            greet_seq(x0)
-            greet_seq(y0)
-
-        seq_peers = 3 + 2 * core
+            pl.semaphore_wait(barrier, 3)
+            tell_partner()
+
+        @pl.when(core == 0)
+        def _():
+            pl.semaphore_wait(go, 1)
     else:
-        each(1, chips, lambda j: greet_seq(peer(j)))
-        seq_peers = chips
-    if line:
-        greet_tp(mirror(2))
-        greet_tp(mirror(1 - inner))
-
-        @pl.when(inner == 1)
-        def _():
-            greet_tp(mirror(3))
-
-        tp_peers = 2 + inner
-    else:
-        for j in range(1, tp):
-            greet_tp((mt + j) % tp)
-        tp_peers = tp - 1
+        greet_seq(partner)
+        if square:
+            for s in (x0, x1, y0, y1):
+                greet_seq(s)
+            seq_peers = 5
+        else:
+            each(1, chips, lambda j: greet_seq(peer(j)))
+            seq_peers = chips
+        if line:
+            greet_tp(mirror(2))
+            greet_tp(mirror(1 - inner))
+
+            @pl.when(inner == 1)
+            def _():
+                greet_tp(mirror(3))
+
+            tp_peers = 2 + inner
+        else:
+            for j in range(1, tp):
+                greet_tp((mt + j) % tp)
+            tp_peers = tp - 1
+        pl.semaphore_wait(barrier, seq_peers + tp_peers)
 
     pltpu.make_async_copy(kv_buf.at[me], kv_buf.at[me], in_sem.at[4]).wait()
-    pl.semaphore_wait(barrier, seq_peers + tp_peers)
 
     def copy(ref, recv_sem, target, turn=0):
         return pltpu.make_async_remote_copy(
@@ -123,11 +147,11 @@
     def slot(s, target):
         return copy(kv_buf.at[s], kv_recv.at[s], target)
 
-    def near_sem(axis, c, g, i):
-        return kv_recv.at[((axis * 2 + c) * kv_heads + g) * 2 + i]
+    def near_sem(axis, c, g):
+        return kv_recv.at[(axis * 2 + c) * kv_heads + g]
 
     def far_sem(c, g, i):
-        return kv_recv.at[(c * kv_heads + g) * 2 + i]
+        return kv_recv.at[((2 + c) * kv_heads + g) * 2 + i]
 
     def several(slots, recv_sem, turn=0):
         return copy(kv_buf.at[pl.ds(0, slots)], recv_sem, partner, turn)
@@ -136,10 +160,13 @@
         for g in heads:
             for i in range(2):
                 copy(kv_buf.at[me, g, i], hop_recv.at[0], partner).start()
-        for i in range(2):
+
+        def send_near(i, x, y):
             for g in heads:
-                copy(kv_buf.at[me, g, i], near_sem(0, core, g, i), x1).start()
-                copy(kv_buf.at[me, g, 1 - i], near_sem(1, core, g, 1 - i), y1).start()
+                copy(kv_buf.at[me, g, i], near_sem(0, core, g), x).start()
+                copy(kv_buf.at[me, g, 1 - i], near_sem(1, core, g), y).start()
+
+        send_near(0, x1, y1)
     else:
         slot(me, partner).start()
         each(1, chips, lambda j: slot(me, peer(j)).start())
@@ -194,7 +221,18 @@
             den[g] = den[g] * fade + added[HEAD:HEAD + 8]
         top_ref[g] = new_top
 
+    if split:
+        @pl.when(core == 0)
+        def _():
+            pl.semaphore_wait(barrier, 2 + 2 * (2 + inner))
+            tell_partner()
+
+        @pl.when(core == 1)
+        def _():
+            pl.semaphore_wait(go, 1)
+
     if square:
+        send_near(1, x0, y0)
         several(1, hop_recv.at[0]).wait_recv()
     else:
         slot(partner, partner).wait_recv()
@@ -215,28 +253,23 @@
         def _():
             for g in heads:
                 for c, sx, sy in ((1, x1, y1), (0, x0, y0)):
-                    arrive(sx, g, 0, near_sem(0, c, g, 0), y0, far_sem(c, g, 0))
-                    arrive(sy, g, 1, near_sem(1, c, g, 1), x0, far_sem(c, g, 1))
+                    arrive(sx, g, 0, near_sem(0, c, g), y0, far_sem(c, g, 0))
+                    arrive(sy, g, 1, near_sem(1, c, g), x0, far_sem(c, g, 1))
+            for g in heads:
+                several(2, hop_recv.at[1 + g]).wait_recv()
+                attend(g, near + far)
+
+        @pl.when(core == 0)
+        def _():
             for g in heads:
                 for c, sx, sy in ((1, x1, y1), (0, x0, y0)):
-                    arrive(sx, g, 1, near_sem(0, c, g, 1))
-                    arrive(sy, g, 0, near_sem(1, c, g, 0))
-                attend(g, near)
-            for g in heads:
-                several(1, hop_recv.at[1 + g]).wait_recv()
-                attend(g, far)
-
-        @pl.when(core == 0)
-        def _():
-            for g in heads:
-                several(2, hop_recv.at[1 + g]).wait_recv()
-                last = g == kv_heads - 1
-                if not last:
-                    attend(g, near)
+                    arrive(sx, g, 1, near_sem(0, c, g))
+                    arrive(sy, g, 0, near_sem(1, c, g))
                 for c, s in ((1, d1), (0, d0)):
                     for i in range(2):
                         arrive(s, g, i, far_sem(c, g, i))
-                attend(g, near + far if last else far)
+                several(1, hop_recv.at[1 + g]).wait_recv()
+                attend(g, near + far)
     else:
         def step(j):
             s = ((chip - j + chips) % chips) * 2 + core
@@ -281,14 +314,7 @@
     def drain():
         if square:
             several(3, hop_recv.at[0]).wait_send()
-
-            @pl.when(core == 1)
-            def _():
-                several(6, hop_recv.at[0], 1).wait_send()
-
-            @pl.when(core == 0)
-            def _():
-                several(2, hop_recv.at[0], 1).wait_send()
+            several(4, hop_recv.at[0], 1).wait_send()
         else:
             several(n - 1, hop_recv.at[0]).wait_send()
 
@@ -310,8 +336,15 @@
         def _():
             send_product(0, m3, relay, 0, lambda i: r_recv.at[0, i], m1)
             send_product(1, m2, relay, 1, lambda i: r_recv.at[1, i], m1)
+            keep_own()
+
+        @pl.when(jnp.logical_and(inner == 0, core == 0))
+        def _():
+            whole_part(1, 0).wait_send()
+
+        @pl.when(inner == 0)
+        def _():
             send_product(2, m1, got, 0, lambda i: g_recv.at[0], m1)
-            keep_own()
 
         @pl.when(inner == 1)
         def _():
@@ -331,7 +364,10 @@
         whole_part(2, 0).wait_recv()
         for b in range(blocks):
             mine[0, b] = mine[0, b] + got[0, b].astype(F32)
-        whole_part(1 + inner, 0).wait_send()
+        @pl.when(jnp.logical_or(inner == 1, core == 1))
+        def _():
+            whole_part(1 + inner, 0).wait_send()
+
         for i in range(pieces):
             b, r = i // 2, slice(i % 2 * half, (i % 2 + 1) * half)
             send_part(2, i, got, 1, f_recv.at[i], m0).wait_recv()
@@ -395,6 +431,7 @@
                 pltpu.VMEM((n_got, blocks, rows, pcols), BF16),
                 dma((5,)), dma((2,)), dma((max(n, 8 * kv_heads) if n == 8 else n,)), dma((1 + kv_heads,)),
                 dma((n_parts,)), dma((2, 2 * blocks)), dma((n_got,)), dma((2 * blocks,)),
+                pltpu.SemaphoreType.REGULAR,
             ],
             compiler_params=pltpu.CompilerParams(
                 collective_id=0, has_side_effects=True, vmem_limit_bytes=48 << 20,

time: 23 us -> 22.6 us (0.983)
  Pallas kernels: 22.2 us -> 21.8 us
    pallas_call x1, Pallas kernels: 22.2 us -> 21.8 us  [per_device(): pl.pallas_call(functools.partial(kernel, n, tp), out_shape=pltpu.VMEM((ro...]
where the time goes in v4:
time: 22.6 us; the launch traced here: 22.5 us
  Pallas kernels  21.8 us (96%)
  local copies, waits for them, and re-layouts  0.66 us (3%)
    pallas_call x1, Pallas kernels, per_device(): pl.pallas_call(functools.partial(kernel, n, tp), out_shape=pltpu.VMEM((ro...  21.8 us
    unnamed x1, local copies, waits for them, and re-layouts  0.66 us

profile of v4, /device:TPU:9, one launch (start us, length us, event | category | flops | bytes accessed | tf_op | source)
XLA Modules:
  0.0 22.5 jit_solution(7295613424656793701)
XLA Ops:
  0.0 21.8 %shard_map.55 = bf16[128,512]{1,0:T(8,128)(2,1)S(1)} custom-call(bf16[128,1024]{1,0:T(8,128)(2,1)} %q_hbm.1, bf16[2,128,256]{2,1,0:T(8,128)(2,1)} %kv_hbm.1, s32[8]{0:T(128)} %order_hbm.1, s32[8,8]{1,0:T(8,128)} %table_hbm.1, bf16[1024,2048]{1,0:T(8,128)(2,1)} %w_hbm.1), custom_call_target="tpu_custom_call" | custom-call | tf_op jit(solution)/shard_map/pallas_call | solution.py:412
  21.8 0.7 %copy.7 = bf16[128,512]{1,0:T(8,128)(2,1)} copy(bf16[128,512]{1,0:T(8,128)(2,1)S(1)} %shard_map.55) | data formatting | bytes 262144

commit v5 on v4

--- a/solution.py
+++ b/solution.py
@@ -138,35 +138,35 @@
 
     pltpu.make_async_copy(kv_buf.at[me], kv_buf.at[me], in_sem.at[4]).wait()
 
-    def copy(ref, recv_sem, target, turn=0):
+    def copy(ref, recv_sem, target):
         return pltpu.make_async_remote_copy(
-            src_ref=ref, dst_ref=ref, send_sem=kv_send.at[turn], recv_sem=recv_sem,
+            src_ref=ref, dst_ref=ref, send_sem=kv_send, recv_sem=recv_sem,
             device_id={"seq": target}, device_id_type=MESH,
         )
 
     def slot(s, target):
         return copy(kv_buf.at[s], kv_recv.at[s], target)
 
-    def near_sem(axis, c, g):
+    def relay_sem(axis, c, g):
         return kv_recv.at[(axis * 2 + c) * kv_heads + g]
 
-    def far_sem(c, g, i):
-        return kv_recv.at[((2 + c) * kv_heads + g) * 2 + i]
-
-    def several(slots, recv_sem, turn=0):
-        return copy(kv_buf.at[pl.ds(0, slots)], recv_sem, partner, turn)
+    def near_sem(g):
+        return kv_recv.at[g]
+
+    def far_sem(g):
+        return kv_recv.at[kv_heads + g]
+
+    def several(slots, recv_sem):
+        return copy(kv_buf.at[pl.ds(0, slots)], recv_sem, partner)
 
     if square:
         for g in heads:
             for i in range(2):
                 copy(kv_buf.at[me, g, i], hop_recv.at[0], partner).start()
 
-        def send_near(i, x, y):
-            for g in heads:
-                copy(kv_buf.at[me, g, i], near_sem(0, core, g), x).start()
-                copy(kv_buf.at[me, g, 1 - i], near_sem(1, core, g), y).start()
-
-        send_near(0, x1, y1)
+        for g in heads:
+            copy(kv_buf.at[me, g, 0], relay_sem(0, core, g), x1).start()
+            copy(kv_buf.at[me, g, 1], relay_sem(1, core, g), y1).start()
     else:
         slot(me, partner).start()
         each(1, chips, lambda j: slot(me, peer(j)).start())
@@ -232,7 +232,9 @@
             pl.semaphore_wait(go, 1)
 
     if square:
-        send_near(1, x0, y0)
+        for g in heads:
+            copy(kv_buf.at[me, g, 1], near_sem(g), x0).start()
+            copy(kv_buf.at[me, g, 0], near_sem(g), y0).start()
         several(1, hop_recv.at[0]).wait_recv()
     else:
         slot(partner, partner).wait_recv()
@@ -242,34 +244,38 @@
     if square:
         near, far = [x1, y1, x0, y0], [d1, d0]
 
-        def arrive(s, g, i, sem, onward=None, onward_sem=None):
-            ref = kv_buf.at[s, g, i]
-            copy(ref, sem, partner).wait_recv()
-            if onward is not None:
-                copy(ref, onward_sem, onward, 1).start()
-            copy(ref, hop_recv.at[1 + g], partner, 1).start()
+        def hand_over(s, g, i, hop):
+            copy(kv_buf.at[s, g, i], hop_recv.at[hop], partner).start()
 
         @pl.when(core == 1)
         def _():
             for g in heads:
                 for c, sx, sy in ((1, x1, y1), (0, x0, y0)):
-                    arrive(sx, g, 0, near_sem(0, c, g), y0, far_sem(c, g, 0))
-                    arrive(sy, g, 1, near_sem(1, c, g), x0, far_sem(c, g, 1))
+                    for axis, s, target in ((0, sx, y0), (1, sy, x0)):
+                        ref = kv_buf.at[s, g, axis]
+                        copy(ref, relay_sem(axis, c, g), partner).wait_recv()
+                        copy(ref, far_sem(g), target).start()
+                        hand_over(s, g, axis, 1 + g)
+            for slots, hop in ((near, 1), (far, 1 + kv_heads)):
+                for g in heads:
+                    several(1, hop_recv.at[hop + g]).wait_recv()
+                    attend(g, slots)
+
+        @pl.when(core == 0)
+        def _():
             for g in heads:
-                several(2, hop_recv.at[1 + g]).wait_recv()
-                attend(g, near + far)
-
-        @pl.when(core == 0)
-        def _():
+                several(1, near_sem(g)).wait_recv()
+                for sx, sy in ((x1, y1), (x0, y0)):
+                    hand_over(sx, g, 1, 1 + g)
+                    hand_over(sy, g, 0, 1 + g)
+                several(1, hop_recv.at[1 + g]).wait_recv()
+                attend(g, near)
             for g in heads:
-                for c, sx, sy in ((1, x1, y1), (0, x0, y0)):
-                    arrive(sx, g, 1, near_sem(0, c, g))
-                    arrive(sy, g, 0, near_sem(1, c, g))
-                for c, s in ((1, d1), (0, d0)):
+                several(1, far_sem(g)).wait_recv()
+                for s in far:
                     for i in range(2):
-                        arrive(s, g, i, far_sem(c, g, i))
-                several(1, hop_recv.at[1 + g]).wait_recv()
-                attend(g, near + far)
+                        hand_over(s, g, i, 1 + kv_heads + g)
+                attend(g, far)
     else:
         def step(j):
             s = ((chip - j + chips) % chips) * 2 + core
@@ -295,8 +301,13 @@
         cols = pl.ds(pl.multiple_of(t * width + b * pcols, pcols), pcols)
         return jnp.dot(att[...], w_buf[:, cols], preferred_element_type=F32)
 
+    cuts = [(b, r * half, half) for b in range(blocks) for r in range(2)]
+    b, r, count = cuts.pop()
+    cuts += [(b, r, count // 2), (b, r + count // 2, count // 2)]
+
     def part_of(ref, slot, i):
-        return ref.at[slot, i // 2, pl.ds(i % 2 * half, half)]
+        b, r, count = cuts[i]
+        return ref.at[slot, b, pl.ds(r, count)]
 
     def send_part(c, i, dst, slot, recv_sem, target):
         return pltpu.make_async_remote_copy(
@@ -313,20 +324,20 @@
 
     def drain():
         if square:
-            several(3, hop_recv.at[0]).wait_send()
-            several(4, hop_recv.at[0], 1).wait_send()
+            several(7, hop_recv.at[0]).wait_send()
         else:
             several(n - 1, hop_recv.at[0]).wait_send()
 
-    pieces = 2 * blocks
+    pieces = len(cuts)
     if line:
         m0, m1, m2, m3 = (mirror(d) for d in range(4))
 
         def send_product(c, t, dst, slot, recv_sems, target):
             for b in range(blocks):
                 parts[c, b] = project(t, b).astype(BF16)
-                for i in (2 * b, 2 * b + 1):
-                    send_part(c, i, dst, slot, recv_sems(i), target).start()
+                for i in range(pieces):
+                    if cuts[i][0] == b:
+                        send_part(c, i, dst, slot, recv_sems(i), target).start()
 
         def keep_own():
             for b in range(blocks):
@@ -354,7 +365,7 @@
                     mine[c, b] = project(t, b)
             for c, target in ((0, m3), (1, m2)):
                 for i in range(pieces):
-                    b, r = i // 2, slice(i % 2 * half, (i % 2 + 1) * half)
+                    b, r = cuts[i][0], pl.ds(*cuts[i][1:])
                     send_part(2, i, relay, c, r_recv.at[c, i], m0).wait_recv()
                     parts[c, b, r] = (mine[1 + c, b, r] + relay[c, b, r].astype(F32)).astype(BF16)
                     send_part(c, i, got, 1, f_recv.at[i], target).start()
@@ -369,7 +380,7 @@
             whole_part(1 + inner, 0).wait_send()
 
         for i in range(pieces):
-            b, r = i // 2, slice(i % 2 * half, (i % 2 + 1) * half)
+            b, r = cuts[i][0], pl.ds(*cuts[i][1:])
             send_part(2, i, got, 1, f_recv.at[i], m0).wait_recv()
             out_ref[r, b * pcols:(b + 1) * pcols] = (mine[0, b, r] + got[1, b, r].astype(F32)).astype(BF16)
         whole_part(2 - inner, 0).wait_send()
@@ -379,8 +390,9 @@
             t = (mt + j) % tp
             for b in range(blocks):
                 parts[j, b] = project(t, b).astype(BF16)
-                for i in (2 * b, 2 * b + 1):
-                    send_part(j, i, got, mt, g_recv.at[mt], t).start()
+                for i in range(pieces):
+                    if cuts[i][0] == b:
+                        send_part(j, i, got, mt, g_recv.at[mt], t).start()
         for b in range(blocks):
             mine[0, b] = project(mt, b)
         drain()
@@ -429,8 +441,8 @@
                 pltpu.VMEM((n_parts, blocks, rows, pcols), BF16),
                 pltpu.VMEM((2, blocks, rows, pcols), BF16),
                 pltpu.VMEM((n_got, blocks, rows, pcols), BF16),
-                dma((5,)), dma((2,)), dma((max(n, 8 * kv_heads) if n == 8 else n,)), dma((1 + kv_heads,)),
-                dma((n_parts,)), dma((2, 2 * blocks)), dma((n_got,)), dma((2 * blocks,)),
+                dma((5,)), dma(()), dma((4 * kv_heads if n == 8 else n,)), dma((1 + 2 * kv_heads,)),
+                dma((n_parts,)), dma((2, 2 * blocks + 1)), dma((1 if line else tp,)), dma((2 * blocks + 1,)),
                 pltpu.SemaphoreType.REGULAR,
             ],
             compiler_params=pltpu.CompilerParams(

time: 22.6 us -> 22.2 us (0.982)
  Pallas kernels: 21.8 us -> 21.4 us
    pallas_call x1, Pallas kernels: 21.8 us -> 21.4 us  [per_device(): pl.pallas_call(functools.partial(kernel, n, tp), out_shape=pltpu.VMEM((ro...]
where the time goes in v5:
time: 22.2 us; the launch traced here: 22 us
  Pallas kernels  21.4 us (96%)
  local copies, waits for them, and re-layouts  0.66 us (3%)
    pallas_call x1, Pallas kernels, per_device(): pl.pallas_call(functools.partial(kernel, n, tp), out_shape=pltpu.VMEM((ro...  21.4 us
    unnamed x1, local copies, waits for them, and re-layouts  0.66 us

profile of v5, /device:TPU:9, one launch (start us, length us, event | category | flops | bytes accessed | tf_op | source)
XLA Modules:
  0.0 22.0 jit_solution(11945758425139497541)
XLA Ops:
  0.0 21.4 %shard_map.55 = bf16[128,512]{1,0:T(8,128)(2,1)S(1)} custom-call(bf16[128,1024]{1,0:T(8,128)(2,1)} %q_hbm.1, bf16[2,128,256]{2,1,0:T(8,128)(2,1)} %kv_hbm.1, s32[8]{0:T(128)} %order_hbm.1, s32[8,8]{1,0:T(8,128)} %table_hbm.1, bf16[1024,2048]{1,0:T(8,128)(2,1)} %w_hbm.1), custom_call_target="tpu_custom_call" | custom-call | tf_op jit(solution)/shard_map/pallas_call | solution.py:424
  21.4 0.7 %copy.7 = bf16[128,512]{1,0:T(8,128)(2,1)} copy(bf16[128,512]{1,0:T(8,128)(2,1)S(1)} %shard_map.55) | data formatting | bytes 262144

commit v6 on v5

--- a/solution.py
+++ b/solution.py
@@ -160,13 +160,13 @@
         return copy(kv_buf.at[pl.ds(0, slots)], recv_sem, partner)
 
     if square:
+
+        for g in heads:
+            copy(kv_buf.at[me, g, 0], relay_sem(0, core, g), x1).start()
+            copy(kv_buf.at[me, g, 1], relay_sem(1, core, g), y1).start()
         for g in heads:
             for i in range(2):
                 copy(kv_buf.at[me, g, i], hop_recv.at[0], partner).start()
-
-        for g in heads:
-            copy(kv_buf.at[me, g, 0], relay_sem(0, core, g), x1).start()
-            copy(kv_buf.at[me, g, 1], relay_sem(1, core, g), y1).start()
     else:
         slot(me, partner).start()
         each(1, chips, lambda j: slot(me, peer(j)).start())
@@ -231,17 +231,37 @@
         def _():
             pl.semaphore_wait(go, 1)
 
+    def begin():
+        for g in heads:
+            attend(g, [me, partner], True)
+
+    def normalise(g):
+        share = 1.0 / den[g][0:1]
+        for j in range(group):
+            h = g * group + j
+            cols = slice(j * rows, (j + 1) * rows)
+            att[:, h * HEAD:(h + 1) * HEAD] = (acc[g, :, cols] * share[:, cols]).astype(BF16).T
+
+    last = kv_heads - 1
+    done = last * group * HEAD
+    early = split and done > 0
+    first_part = mirror(3) * (1 - inner) + mirror(0) * inner
+
+    def columns(t):
+        return pl.ds(pl.multiple_of(t * width, width), width)
+
+    def look_ahead(g):
+        if early and g == last:
+            for k in range(last):
+                normalise(k)
+            ahead = jnp.dot(att[:, :done], w_buf[:done, columns(first_part)], preferred_element_type=F32)
+            for b in range(blocks):
+                mine[0, b] = ahead[:, b * pcols:(b + 1) * pcols]
+
     if square:
         for g in heads:
             copy(kv_buf.at[me, g, 1], near_sem(g), x0).start()
             copy(kv_buf.at[me, g, 0], near_sem(g), y0).start()
-        several(1, hop_recv.at[0]).wait_recv()
-    else:
-        slot(partner, partner).wait_recv()
-    for g in heads:
-        attend(g, [me, partner], True)
-
-    if square:
         near, far = [x1, y1, x0, y0], [d1, d0]
 
         def hand_over(s, g, i, hop):
@@ -256,13 +276,21 @@
                         copy(ref, relay_sem(axis, c, g), partner).wait_recv()
                         copy(ref, far_sem(g), target).start()
                         hand_over(s, g, axis, 1 + g)
+            several(1, hop_recv.at[0]).wait_recv()
+            begin()
+            load_w.wait()
             for slots, hop in ((near, 1), (far, 1 + kv_heads)):
                 for g in heads:
                     several(1, hop_recv.at[hop + g]).wait_recv()
+                    if slots is far:
+                        look_ahead(g)
                     attend(g, slots)
 
         @pl.when(core == 0)
         def _():
+            several(1, hop_recv.at[0]).wait_recv()
+            begin()
+            load_w.wait()
             for g in heads:
                 several(1, near_sem(g)).wait_recv()
                 for sx, sy in ((x1, y1), (x0, y0)):
@@ -275,8 +303,13 @@
                 for s in far:
                     for i in range(2):
                         hand_over(s, g, i, 1 + kv_heads + g)
+                look_ahead(g)
                 attend(g, far)
     else:
+        slot(partner, partner).wait_recv()
+        begin()
+        load_w.wait()
+
         def step(j):
             s = ((chip - j + chips) % chips) * 2 + core
             other = ((chip - j + chips) % chips) * 2 + 1 - core
@@ -288,22 +321,16 @@
 
         each(1, chips, step)
 
-    for g in heads:
-        share = 1.0 / den[g][0:1]
-        for j in range(group):
-            h = g * group + j
-            cols = slice(j * rows, (j + 1) * rows)
-            att[:, h * HEAD:(h + 1) * HEAD] = (acc[g, :, cols] * share[:, cols]).astype(BF16).T
-
-    load_w.wait()
-
-    def project(t, b):
-        cols = pl.ds(pl.multiple_of(t * width + b * pcols, pcols), pcols)
-        return jnp.dot(att[...], w_buf[:, cols], preferred_element_type=F32)
-
-    cuts = [(b, r * half, half) for b in range(blocks) for r in range(2)]
-    b, r, count = cuts.pop()
-    cuts += [(b, r, count // 2), (b, r + count // 2, count // 2)]
+    for g in [last] if early else heads:
+        normalise(g)
+
+    def project(t, ref, slot, ready=0):
+        product = jnp.dot(att[:, ready:], w_buf[ready:, columns(t)], preferred_element_type=F32)
+        for b in range(blocks):
+            block = product[:, b * pcols:(b + 1) * pcols]
+            ref[slot, b] = (block + mine[0, b] if ready else block).astype(ref.dtype)
+
+    cuts = [(b, r * half // 2, half // 2) for b in range(blocks) for r in range(4)]
 
     def part_of(ref, slot, i):
         b, r, count = cuts[i]
@@ -332,20 +359,17 @@
     if line:
         m0, m1, m2, m3 = (mirror(d) for d in range(4))
 
-        def send_product(c, t, dst, slot, recv_sems, target):
-            for b in range(blocks):
-                parts[c, b] = project(t, b).astype(BF16)
-                for i in range(pieces):
-                    if cuts[i][0] == b:
-                        send_part(c, i, dst, slot, recv_sems(i), target).start()
+        def send_product(c, t, dst, slot, recv_sems, target, ready=0):
+            project(t, parts, c, ready)
+            for i in range(pieces):
+                send_part(c, i, dst, slot, recv_sems(i), target).start()
 
         def keep_own():
-            for b in range(blocks):
-                mine[0, b] = project(mt, b)
+            project(mt, mine, 0)
 
         @pl.when(inner == 0)
         def _():
-            send_product(0, m3, relay, 0, lambda i: r_recv.at[0, i], m1)
+            send_product(0, m3, relay, 0, lambda i: r_recv.at[0, i], m1, done if early else 0)
             send_product(1, m2, relay, 1, lambda i: r_recv.at[1, i], m1)
             keep_own()
 
@@ -359,10 +383,9 @@
 
         @pl.when(inner == 1)
         def _():
-            send_product(2, m0, got, 0, lambda i: g_recv.at[0], m0)
+            send_product(2, m0, got, 0, lambda i: g_recv.at[0], m0, done if early else 0)
             for c, t in ((1, m3), (2, m2), (0, mt)):
-                for b in range(blocks):
-                    mine[c, b] = project(t, b)
+                project(t, mine, c)
             for c, target in ((0, m3), (1, m2)):
                 for i in range(pieces):
                     b, r = cuts[i][0], pl.ds(*cuts[i][1:])
@@ -388,13 +411,10 @@
         ahead = sorted(range(1, tp), key=lambda j: -min(j, tp - j))
         for j in ahead:
             t = (mt + j) % tp
-            for b in range(blocks):
-                parts[j, b] = project(t, b).astype(BF16)
-                for i in range(pieces):
-                    if cuts[i][0] == b:
-                        send_part(j, i, got, mt, g_recv.at[mt], t).start()
-        for b in range(blocks):
-            mine[0, b] = project(mt, b)
+            project(t, parts, j)
+            for i in range(pieces):
+                send_part(j, i, got, mt, g_recv.at[mt], t).start()
+        project(mt, mine, 0)
         drain()
         for j in reversed(ahead):
             source = (mt + j) % tp
@@ -442,7 +462,7 @@
                 pltpu.VMEM((2, blocks, rows, pcols), BF16),
                 pltpu.VMEM((n_got, blocks, rows, pcols), BF16),
                 dma((5,)), dma(()), dma((4 * kv_heads if n == 8 else n,)), dma((1 + 2 * kv_heads,)),
-                dma((n_parts,)), dma((2, 2 * blocks + 1)), dma((1 if line else tp,)), dma((2 * blocks + 1,)),
+                dma((n_parts,)), dma((2, 4 * blocks)), dma((1 if line else tp,)), dma((4 * blocks,)),
                 pltpu.SemaphoreType.REGULAR,
             ],
             compiler_params=pltpu.CompilerParams(

time: 22.2 us -> 22.1 us (level)
  no operation moved by 1% of the time
where the time goes in v6:
time: 22.1 us; the launch traced here: 22 us
  Pallas kernels  21.3 us (96%)
  local copies, waits for them, and re-layouts  0.66 us (3%)
    pallas_call x1, Pallas kernels, per_device(): pl.pallas_call(functools.partial(kernel, n, tp), out_shape=pltpu.VMEM((ro...  21.3 us
    unnamed x1, local copies, waits for them, and re-layouts  0.66 us

profile of v6, /device:TPU:9, one launch (start us, length us, event | category | flops | bytes accessed | tf_op | source)
XLA Modules:
  0.0 22.0 jit_solution(15554329616718220378)
XLA Ops:
  0.0 21.3 %shard_map.55 = bf16[128,512]{1,0:T(8,128)(2,1)S(1)} custom-call(bf16[128,1024]{1,0:T(8,128)(2,1)} %q_hbm.1, bf16[2,128,256]{2,1,0:T(8,128)(2,1)} %kv_hbm.1, s32[8]{0:T(128)} %order_hbm.1, s32[8,8]{1,0:T(8,128)} %table_hbm.1, bf16[1024,2048]{1,0:T(8,128)(2,1)} %w_hbm.1), custom_call_target="tpu_custom_call" | custom-call | tf_op jit(solution)/shard_map/pallas_call | solution.py:444
  21.3 0.7 %copy.7 = bf16[128,512]{1,0:T(8,128)(2,1)} copy(bf16[128,512]{1,0:T(8,128)(2,1)S(1)} %shard_map.55) | data formatting | bytes 262144

commit v7 on v6

--- a/solution.py
+++ b/solution.py
@@ -150,11 +150,14 @@
     def relay_sem(axis, c, g):
         return kv_recv.at[(axis * 2 + c) * kv_heads + g]
 
-    def near_sem(g):
-        return kv_recv.at[g]
-
-    def far_sem(g):
-        return kv_recv.at[kv_heads + g]
+    def near_sem(c, g):
+        return kv_recv.at[c * kv_heads + g]
+
+    def far_sem(c, g):
+        return kv_recv.at[(2 + c) * kv_heads + g]
+
+    def pair(recv_sem):
+        return copy(kv_buf.at[0, 0], recv_sem, partner)
 
     def several(slots, recv_sem):
         return copy(kv_buf.at[pl.ds(0, slots)], recv_sem, partner)
@@ -260,8 +263,8 @@
 
     if square:
         for g in heads:
-            copy(kv_buf.at[me, g, 1], near_sem(g), x0).start()
-            copy(kv_buf.at[me, g, 0], near_sem(g), y0).start()
+            copy(kv_buf.at[me, g, 1], near_sem(core, g), x0).start()
+            copy(kv_buf.at[me, g, 0], near_sem(core, g), y0).start()
         near, far = [x1, y1, x0, y0], [d1, d0]
 
         def hand_over(s, g, i, hop):
@@ -274,7 +277,7 @@
                     for axis, s, target in ((0, sx, y0), (1, sy, x0)):
                         ref = kv_buf.at[s, g, axis]
                         copy(ref, relay_sem(axis, c, g), partner).wait_recv()
-                        copy(ref, far_sem(g), target).start()
+                        copy(ref, far_sem(c, g), target).start()
                         hand_over(s, g, axis, 1 + g)
             several(1, hop_recv.at[0]).wait_recv()
             begin()
@@ -292,15 +295,15 @@
             begin()
             load_w.wait()
             for g in heads:
-                several(1, near_sem(g)).wait_recv()
-                for sx, sy in ((x1, y1), (x0, y0)):
+                for c, sx, sy in ((1, x1, y1), (0, x0, y0)):
+                    pair(near_sem(c, g)).wait_recv()
                     hand_over(sx, g, 1, 1 + g)
                     hand_over(sy, g, 0, 1 + g)
                 several(1, hop_recv.at[1 + g]).wait_recv()
                 attend(g, near)
             for g in heads:
-                several(1, far_sem(g)).wait_recv()
-                for s in far:
+                for c, s in ((1, d1), (0, d0)):
+                    pair(far_sem(c, g)).wait_recv()
                     for i in range(2):
                         hand_over(s, g, i, 1 + kv_heads + g)
                 look_ahead(g)
@@ -356,6 +359,11 @@
             several(n - 1, hop_recv.at[0]).wait_send()
 
     pieces = len(cuts)
+    early_pieces = pieces - 4
+
+    def combined(i):
+        return f_recv.at[max(i - early_pieces + 1, 0)]
+
     if line:
         m0, m1, m2, m3 = (mirror(d) for d in range(4))
 
@@ -391,7 +399,7 @@
                     b, r = cuts[i][0], pl.ds(*cuts[i][1:])
                     send_part(2, i, relay, c, r_recv.at[c, i], m0).wait_recv()
                     parts[c, b, r] = (mine[1 + c, b, r] + relay[c, b, r].astype(F32)).astype(BF16)
-                    send_part(c, i, got, 1, f_recv.at[i], target).start()
+                    send_part(c, i, got, 1, combined(i), target).start()
 
         drain()
         whole_part(0, 0).wait_send()
@@ -402,9 +410,16 @@
         def _():
             whole_part(1 + inner, 0).wait_send()
 
+        if early_pieces:
+            begun = pl.ds(0, blocks - 1)
+            pltpu.make_async_remote_copy(
+                src_ref=got.at[1, begun], dst_ref=got.at[1, begun], send_sem=p_send.at[0],
+                recv_sem=combined(0), device_id={"tp": mt}, device_id_type=MESH,
+            ).wait_recv()
         for i in range(pieces):
             b, r = cuts[i][0], pl.ds(*cuts[i][1:])
-            send_part(2, i, got, 1, f_recv.at[i], m0).wait_recv()
+            if i >= early_pieces:
+                send_part(2, i, got, 1, combined(i), m0).wait_recv()
             out_ref[r, b * pcols:(b + 1) * pcols] = (mine[0, b, r] + got[1, b, r].astype(F32)).astype(BF16)
         whole_part(2 - inner, 0).wait_send()
     else:
@@ -462,7 +477,7 @@
                 pltpu.VMEM((2, blocks, rows, pcols), BF16),
                 pltpu.VMEM((n_got, blocks, rows, pcols), BF16),
                 dma((5,)), dma(()), dma((4 * kv_heads if n == 8 else n,)), dma((1 + 2 * kv_heads,)),
-                dma((n_parts,)), dma((2, 4 * blocks)), dma((1 if line else tp,)), dma((4 * blocks,)),
+                dma((n_parts,)), dma((2, 4 * blocks)), dma((1 if line else tp,)), dma((5,)),
                 pltpu.SemaphoreType.REGULAR,
             ],
             compiler_params=pltpu.CompilerParams(

time: 22.1 us -> 22.1 us (level)
  no operation moved by 1% of the time
where the time goes in v7:
time: 22.1 us; the launch traced here: 22 us
  Pallas kernels  21.3 us (96%)
  local copies, waits for them, and re-layouts  0.66 us (3%)
    pallas_call x1, Pallas kernels, per_device(): pl.pallas_call(functools.partial(kernel, n, tp), out_shape=pltpu.VMEM((ro...  21.3 us
    unnamed x1, local copies, waits for them, and re-layouts  0.66 us

profile of v7, /device:TPU:9, one launch (start us, length us, event | category | flops | bytes accessed | tf_op | source)
XLA Modules:
  0.0 22.0 jit_solution(1446469618420478732)
XLA Ops:
  0.0 21.3 %shard_map.55 = bf16[128,512]{1,0:T(8,128)(2,1)S(1)} custom-call(bf16[128,1024]{1,0:T(8,128)(2,1)} %q_hbm.1, bf16[2,128,256]{2,1,0:T(8,128)(2,1)} %kv_hbm.1, s32[8]{0:T(128)} %order_hbm.1, s32[8,8]{1,0:T(8,128)} %table_hbm.1, bf16[1024,2048]{1,0:T(8,128)(2,1)} %w_hbm.1), custom_call_target="tpu_custom_call" | custom-call | tf_op jit(solution)/shard_map/pallas_call | solution.py:459
  21.3 0.7 %copy.7 = bf16[128,512]{1,0:T(8,128)(2,1)} copy(bf16[128,512]{1,0:T(8,128)(2,1)S(1)} %shard_map.55) | data formatting | bytes 262144

commit v8 on v7

--- a/solution.py
+++ b/solution.py
@@ -381,10 +381,6 @@
             send_product(1, m2, relay, 1, lambda i: r_recv.at[1, i], m1)
             keep_own()
 
-        @pl.when(jnp.logical_and(inner == 0, core == 0))
-        def _():
-            whole_part(1, 0).wait_send()
-
         @pl.when(inner == 0)
         def _():
             send_product(2, m1, got, 0, lambda i: g_recv.at[0], m1)
@@ -406,9 +402,7 @@
         whole_part(2, 0).wait_recv()
         for b in range(blocks):
             mine[0, b] = mine[0, b] + got[0, b].astype(F32)
-        @pl.when(jnp.logical_or(inner == 1, core == 1))
-        def _():
-            whole_part(1 + inner, 0).wait_send()
+        whole_part(1 + inner, 0).wait_send()
 
         if early_pieces:
             begun = pl.ds(0, blocks - 1)

time: 22.1 us -> 22.1 us (level)
  no operation moved by 1% of the time
where the time goes in v8:
time: 22.1 us; the launch traced here: 22 us
  Pallas kernels  21.3 us (96%)
  local copies, waits for them, and re-layouts  0.66 us (3%)
    pallas_call x1, Pallas kernels, per_device(): pl.pallas_call(functools.partial(kernel, n, tp), out_shape=pltpu.VMEM((ro...  21.3 us
    unnamed x1, local copies, waits for them, and re-layouts  0.66 us

profile of v8, /device:TPU:9, one launch (start us, length us, event | category | flops | bytes accessed | tf_op | source)
XLA Modules:
  0.0 22.0 jit_solution(7745153901297938593)
XLA Ops:
  0.0 21.3 %shard_map.55 = bf16[128,512]{1,0:T(8,128)(2,1)S(1)} custom-call(bf16[128,1024]{1,0:T(8,128)(2,1)} %q_hbm.1, bf16[2,128,256]{2,1,0:T(8,128)(2,1)} %kv_hbm.1, s32[8]{0:T(128)} %order_hbm.1, s32[8,8]{1,0:T(8,128)} %table_hbm.1, bf16[1024,2048]{1,0:T(8,128)(2,1)} %w_hbm.1), custom_call_target="tpu_custom_call" | custom-call | tf_op jit(solution)/shard_map/pallas_call | solution.py:453
  21.3 0.7 %copy.7 = bf16[128,512]{1,0:T(8,128)(2,1)} copy(bf16[128,512]{1,0:T(8,128)(2,1)S(1)} %shard_map.55) | data formatting | bytes 262144
